TPU v7x, 32 devices: a whole 2x2x4 slice. The times are simulated.
32 devices in a mesh: tile: 16 (over z, x, core), mem: 2 (over y).
Axes of the slice: x: 2, y: 2, z: 4, core: 2. Of those that a mesh axis runs over, the one named last changes fastest.
Arguments:
- anomalies: bfloat16 [80, 137, 2048], P('mem', None, 'tile'), may hold values from -6 to 6
- analysis_weights: bfloat16 [16, 80, 80], P('tile'), may hold values from -0.6 to 1.7
- background_mean: bfloat16 [137, 2048], P(None, 'tile'), may hold values from -6 to 6
- background: bfloat16 [80, 137, 2048], P('mem', None, 'tile'), may hold values from -6 to 6
- jacobian_table: bfloat16 [8461, 137], replicated, may hold values from -0.5 to 0.5
- channel_list: int32 [96], replicated, may hold values from 0 to 8460
- send_slots: int32 [16, 16, 32], P('tile'), may hold values from -1 to 127, as said below
- footprint: int32 [8192, 4], P('tile'), may hold values from 0 to 511, as said below
- footprint_weight: bfloat16 [8192, 4], P('tile'), may hold values from 0.25 to 1
- channel_bias: float32 [96], replicated, may hold values from -4 to 4
Outputs:
- analysis_members: bfloat16 [80, 137, 2048], P('mem', None, 'tile')
- radiance_prior: float32 [96, 80, 8192], P(None, 'mem', 'tile')
Inputs may be any that keep to these rules, and one draw needn't show every extreme that they name: `send_slots`: entry [s, d, i] is a column within owner s's block of 128 columns that owner s sends to tile d in slot i, or -1 for an empty slot; the filled slots of a pair come first, each pair fills 1 to 32 slots, and in every draw one tile receives 32 filled slots from every owner. `footprint`: entry [o, j] is a slot of the buffer of observation o's tile, which holds 32 slots from each owner in owner order; every entry names a filled slot, the 4 entries of a row differ, and every filled slot is named by some row of that tile.
All inputs are finite; a program needn't handle non-finite values.
Results may differ from a plain program's by a relative error of at most 0.0021.
Values may be sent and summed in bfloat16 or wider, within the bound.
No kernel may reach another device: no remote copies, remote signals or barrier semaphores. Data moves between devices by JAX's collectives and lax.ppermute only.
A program may use at most 128 MiB of HBM per device.

v0:
```python
import functools

import jax
import jax.numpy as jnp
from jax import lax
from jax.experimental import pallas as pl
from jax.experimental.pallas import tpu as pltpu
from jax.sharding import PartitionSpec as P

LANES = 128
SPLIT = (2, 2, 2)


def one_hot(index, count, dtype=jnp.bfloat16):
    return (index[..., None] == lax.iota(jnp.int32, count)).astype(dtype)


def dot(spec, a, b):
    return jnp.einsum(spec, a, b, preferred_element_type=jnp.float32)


def pack_kernel(sends, relays, me_ref, slot_ref, owned_ref, *out_refs):
    columns_dev = owned_ref.shape[1]
    slots = slot_ref.shape[1]
    named = jnp.concatenate(
        [slot_ref[pl.ds(me_ref[0] ^ d, 1), :] for d, _, _ in sends], axis=1
    )
    column = lax.broadcasted_iota(jnp.int32, (columns_dev, named.shape[1]), 0)
    hot = jnp.where(column == named, 1.0, 0.0).T.astype(jnp.bfloat16)
    own = owned_ref[...].T
    for first, stop in dict.fromkeys(send[1:] for send in sends):
        picked = [n for n, send in enumerate(sends) if send[1:] == (first, stop)]
        rows = hot[picked[0] * slots : (picked[-1] + 1) * slots]
        packed = jnp.dot(rows, own[:, first:stop], preferred_element_type=jnp.float32)
        packed = packed.astype(jnp.bfloat16)
        for k, n in enumerate(picked):
            out_refs[n][...] = packed[k * slots : (k + 1) * slots]
    for (first, stop), ref in zip(relays, out_refs[len(sends) :]):
        ref[...] = own[:, first:stop]


def pack(me, send_slots, owned, sends, relays):
    rows, columns_dev = owned.shape
    slots = send_slots.shape[1]
    shapes = [(slots, stop - first) for _, first, stop in sends]
    shapes += [(columns_dev, stop - first) for first, stop in relays]
    outs = pl.pallas_call(
        functools.partial(pack_kernel, sends, relays),
        in_specs=[
            pl.BlockSpec(memory_space=pltpu.SMEM),
            pl.BlockSpec(memory_space=pltpu.VMEM),
            pl.BlockSpec(memory_space=pltpu.VMEM),
        ],
        out_specs=[pl.BlockSpec(memory_space=pltpu.VMEM)] * len(shapes),
        out_shape=[jax.ShapeDtypeStruct(shape, owned.dtype) for shape in shapes],
        cost_estimate=pl.CostEstimate(
            flops=2 * len(sends) * slots * columns_dev * rows,
            bytes_accessed=2 * rows * (2 * columns_dev + len(sends) * slots),
            transcendentals=0,
        ),
        name="pack",
    )(me, send_slots, owned)
    return list(outs[: len(sends)]), list(outs[len(sends) :])


def relay_kernel(hot_ref, *refs):
    start = 0
    for ref in refs[:-1]:
        stop = start + ref.shape[1]
        refs[-1][:, start:stop] = jnp.dot(
            hot_ref[...], ref[...], preferred_element_type=jnp.float32
        ).astype(jnp.bfloat16)
        start = stop


def relay_pack(hot, pieces):
    width = sum(piece.shape[1] for piece in pieces)
    return pl.pallas_call(
        relay_kernel,
        out_shape=jax.ShapeDtypeStruct((hot.shape[0], width), jnp.bfloat16),
        cost_estimate=pl.CostEstimate(
            flops=2 * hot.size * width,
            bytes_accessed=2 * width * sum(hot.shape),
            transcendentals=0,
        ),
        name="relay",
    )(hot, *pieces)


def prior_kernel(
    first, count, block, mem_dev, sources, bias_ref, place_ref, spread_ref, *refs
):
    prior_ref, table_ref, done_ref, sems = refs[-4:]

    start = 0
    for side in range(2):
        rows = spread_ref.shape[0] // 2 // sources[side]
        for d in range(sources[side]):
            at = side * rows * sources[side]
            if sources[side] > 1:
                at = pl.multiple_of(at + (place_ref[0] ^ d) * rows, rows)
            table_ref[start : start + rows] = spread_ref[pl.ds(at, rows)]
            start += rows

    width = block * mem_dev
    copies = []
    for i in range(count):
        lanes = slice(i * width, (i + 1) * width)
        rows = jnp.concatenate([ref[:, lanes] for ref in refs[: sum(sources)]], axis=0)
        total = lax.dot_general(
            rows,
            table_ref[...],
            (((0,), (0,)), ((), ())),
            preferred_element_type=jnp.float32,
        )
        for c in range(block):
            bias = bias_ref[(first + i) * block + c]
            done_ref[i, c] = total[c * mem_dev : (c + 1) * mem_dev] + bias
        copies.append(
            pltpu.make_async_copy(
                done_ref.at[i],
                prior_ref.at[pl.ds((first + i) * block, block)],
                sems.at[i],
            )
        )
        copies[-1].start()
    for copy in copies:
        copy.wait()


def prior_piece(shape, block, first, count, near, far, spread, bias, place, so_far):
    _, mem_dev, obs_count = shape
    width = count * block * mem_dev
    slots, all_slots = near[0].shape[0], spread.shape[0]
    in_specs = [
        pl.BlockSpec(memory_space=pltpu.SMEM),
        pl.BlockSpec(memory_space=pltpu.SMEM),
        pl.BlockSpec(memory_space=pltpu.VMEM),
        *[pl.BlockSpec((slots, width), lambda i: (0, first // count))] * len(near),
        *[pl.BlockSpec(memory_space=pltpu.VMEM)] * len(far),
    ]
    operands = [bias, place, spread, *near, *far]
    aliases = {}
    if so_far is not None:
        aliases = {len(operands): 0}
        in_specs.append(pl.BlockSpec(memory_space=pl.ANY))
        operands.append(so_far)
    return pl.pallas_call(
        functools.partial(
            prior_kernel, first, count, block, mem_dev, (len(near), len(far))
        ),
        grid=(1,),
        in_specs=in_specs,
        out_specs=pl.BlockSpec(memory_space=pl.ANY),
        out_shape=jax.ShapeDtypeStruct(shape, jnp.float32),
        scratch_shapes=[
            pltpu.VMEM(spread.shape, spread.dtype),
            pltpu.VMEM((count, block, mem_dev, obs_count), jnp.float32),
            pltpu.SemaphoreType.DMA((count,)),
        ],
        input_output_aliases=aliases,
        cost_estimate=pl.CostEstimate(
            flops=2 * all_slots * width * obs_count,
            bytes_accessed=2 * width * (all_slots + 2 * obs_count),
            transcendentals=0,
        ),
        name="prior",
    )(*operands)


def pieces_of(channels, mem_dev):
    for block in range(1, channels // 2 + 1):
        if channels % block == 0 and block * mem_dev % LANES == 0:
            if sum(SPLIT) * block == channels:
                return block, SPLIT
            return block, (channels // block, 0)
    return channels, (1, 0)


def shards(
    n_tile,
    n_mem,
    anomalies,
    analysis_weights,
    background_mean,
    background,
    jacobian_table,
    channel_list,
    send_slots,
    footprint,
    footprint_weight,
    channel_bias,
):
    mem_dev, _, columns_dev = anomalies.shape
    spectrum = jacobian_table.shape[0]
    channels = channel_list.shape[0]
    slots = send_slots.shape[2]
    obs_count, foot = footprint.shape
    half = n_tile // 2
    half_slots = half * slots
    me = lax.axis_index("tile")
    mine = lax.axis_index("mem")
    my_half = me // half
    halves = [[h * half + i for i in range(half)] for h in range(2)]
    mirror = [(i, (i + half) % n_tile) for i in range(n_tile)]
    block, split = pieces_of(channels, mem_dev)
    relay, direct = sum(split[:-1]), split[-1]

    place = me % half
    far_cols = lax.dynamic_slice_in_dim(send_slots[0], (1 - my_half) * half, half, 0)
    relay_cols = lax.ppermute(far_cols, "tile", mirror)

    picks = one_hot(channel_list, spectrum)
    selected = dot("cs,sl->cl", picks, jacobian_table).astype(jnp.bfloat16)
    selected = lax.optimization_barrier(selected)
    owned = dot("cl,klx->ckx", selected, background).astype(jnp.bfloat16)
    owned = owned.reshape(channels * mem_dev, columns_dev)
    relay_hot = lax.optimization_barrier(one_hot(relay_cols.reshape(-1), columns_dev))

    def to_partner(array, d):
        return lax.ppermute(array, "tile", [(i, i ^ d) for i in range(n_tile)])

    windows, first = [], 0
    for count in split:
        windows.append((first, first + count * block * mem_dev))
        first = windows[-1][1]
    total = first
    args = me[None], send_slots[0], owned
    early = range(half // 2, half)
    late = [d for d in range(half) if d not in early]
    direct_to = range(half, n_tile) if direct else ()
    near = [None] * half
    sent, seen = pack(*args, [(d, 0, total) for d in early], windows[:1])
    for d, array in zip(early, sent):
        near[d] = array
    sent, more = pack(
        *args,
        [(d, 0, total) for d in late] + [(d, *windows[-1]) for d in direct_to],
        windows[1:-1],
    )
    for d, array in zip(late, sent):
        near[d] = array
    far = sent[len(late) :]
    seen = seen + more
    for i in range(len(seen)):
        seen[i] = lax.ppermute(seen[i], "tile", mirror)
    near[1:] = [to_partner(near[d], d) for d in range(1, half)]
    far = [to_partner(far[d], half + d) for d in range(len(far))]

    places = footprint.T
    weights = footprint_weight.T
    near_place = places - my_half * half_slots
    far_place = places - (1 - my_half) * half_slots
    mixed_place = jnp.stack([near_place, far_place])
    spread = sum(
        jnp.where(
            mixed_place[:, None, j] == lax.iota(jnp.int32, half_slots)[None, :, None],
            weights[j],
            jnp.zeros((), weights.dtype),
        )
        for j in range(foot)
    ).reshape(2 * half_slots, obs_count)

    shape = (channels, mem_dev, obs_count)
    relayed = relay_pack(relay_hot, seen)
    relayed = lax.all_to_all(
        relayed, "tile", 0, 0, tiled=True, axis_index_groups=halves
    )
    prior = None
    for first, count, others in ((relay, direct, far), (0, relay, [relayed])):
        if count:
            prior = prior_piece(
                shape, block, first, count, near, others,
                spread, channel_bias, place[None], prior,
            )

    weight_cols = lax.dynamic_slice_in_dim(analysis_weights[0], mine * mem_dev, mem_dev, 1)
    mixture = background_mean.astype(jnp.float32)[None]
    for shift in range(n_mem):
        piece = anomalies
        if shift:
            piece = lax.ppermute(
                anomalies, "mem", [((i + shift) % n_mem, i) for i in range(n_mem)]
            )
        start = lax.rem(mine + shift, n_mem) * mem_dev
        part = lax.dynamic_slice_in_dim(weight_cols, start, mem_dev, 0)
        mixture = mixture + dot("klc,km->mlc", piece, part)
    mixture = mixture.astype(jnp.bfloat16)
    return mixture, prior


def solution(mesh):
    sizes = dict(mesh.shape)
    placed = (
        P("mem", None, "tile"),
        P("tile", None, None),
        P(None, "tile"),
        P("mem", None, "tile"),
        P(),
        P(),
        P("tile", None, None),
        P("tile", None),
        P("tile", None),
        P(),
    )

    def body(*arrays):
        return shards(sizes["tile"], sizes["mem"], *arrays)

    return jax.shard_map(
        body,
        mesh=mesh,
        in_specs=placed,
        out_specs=(P("mem", None, "tile"), P(None, "mem", "tile")),
        check_vma=False,
    )
```

profile of v0, /device:TPU:11, one launch (start us, length us, event | category | flops | bytes accessed | tf_op | source)
XLA Modules:
  0.0 135.8 jit_solution(6910684672961079834)
XLA Ops:
  0.7 1.7 %copy-done = bf16[8461,137]{0,1:T(8,128)(2,1)S(1)} copy-done((bf16[8461,137]{0,1:T(8,128)(2,1)S(1)}, bf16[8461,137]{0,1:T(8,128)(2,1)}, u32[]{:S(2)}) %copy-start) | copy-done | bytes 2318338
  2.3 1.6 %fusion.7 = bf16[96,137]{0,1:T(8,128)(2,1)S(1)} fusion(bf16[8461,137]{0,1:T(8,128)(2,1)S(1)} %copy-done, s32[96]{0:T(128)} %param.15), kind=kOutput, calls=%fused_computation.7 | convolution fusion | flops 223383552 | bytes 2345002 | tf_op jit(solution)/shard_map/cs,sl->cl/dot_general | solution.py:19
  4.5 1.3 copy.16
  5.8 3.1 %pack.2 = (bf16[32,3840]{1,0:T(8,128)(2,1)}, bf16[32,3840]{1,0:T(8,128)(2,1)}, bf16[32,3840]{1,0:T(8,128)(2,1)}, bf16[32,3840]{1,0:T(8,128)(2,1)}, bf16[32,1280]...) custom-call(s32[1]{0:T(128)} %bitcast.14.me_ref, ...), custom_call_target="tpu_custom_call" | custom-call | flops 377487360 | bytes 4915200 | tf_op jit(solution)/shard_map/pack/pallas_call | solution.py:47
  8.9 2.3 %collective-permute-start.10 = (bf16[128,1280]{1,0:T(8,128)(2,1)}, bf16[128,1280]{1,0:T(8,128)(2,1)S(1)}, u32[]{:S(2)}, u32[]{:S(2)}) collective-permute-start(bf16[128,1280]{1,0:T(8,128)(2,1)} %get-tuple-element.29), channel_id=1, source_target_pairs={{0,16},{2,18},{4,20},{6,22},{8,24},{10,26},{12,28},{14,30},{16,0},... | collective-permute-start | bytes 983048 | tf_op jit(solution)/shard_map/ppermute | solution.py:246
  11.2 2.9 %pack.3 = (bf16[32,3840]{1,0:T(8,128)(2,1)}, bf16[32,3840]{1,0:T(8,128)(2,1)}, bf16[32,3840]{1,0:T(8,128)(2,1)}, bf16[32,3840]{1,0:T(8,128)(2,1)}, bf16[128,1280]{1,0:T(8,128)(2,1)}) custom-call(s32[1]{0:T(128)} %bitcast.14.me_ref, s32[16,32]{1,0:T(8,128)} %bitcast.76, bf16[3840,128]{1,0:T(8,128)(2,1)} %bitcast.74), custom_call_target="tpu_custom_call" | custom-call | flops 125829120 | bytes 2949120 | tf_op jit(solution)/shard_map/pack/pallas_call | solution.py:47
  14.1 2.3 %collective-permute-start.8 = (s32[8,32]{1,0:T(8,128)S(1)}, s32[8,32]{1,0:T(8,128)S(1)}, u32[]{:S(2)}, u32[]{:S(2)}) collective-permute-start(s32[8,32]{1,0:T(8,128)S(1)} %dynamic-slice_bitcast_fusion), channel_id=1, source_target_pairs={{0,16},{2,18},{4,20},{6,22},{8,24},{10,26},{12,28},{14,30},{16,0},... | collective-permute-start | bytes 3080 | tf_op jit(solution)/shard_map/ppermute | solution.py:211
  16.4 23.5 %collective-permute-done.8 = s32[8,32]{1,0:T(8,128)S(1)} collective-permute-done((s32[8,32]{1,0:T(8,128)S(1)}, s32[8,32]{1,0:T(8,128)S(1)}, u32[]{:S(2)}, u32[]{:S(2)}) %collective-permute-start.8) | collective-permute-done | bytes 1056 | tf_op jit(solution)/shard_map/ppermute | solution.py:211
  42.2 2.7 %relay.1 = bf16[256,2560]{1,0:T(8,128)(2,1)} custom-call(bf16[256,128]{1,0:T(8,128)(2,1)} %fusion.15.hot_ref, bf16[128,1280]{1,0:T(8,128)(2,1)} %copy-done.7, bf16[128,1280]{1,0:T(8,128)(2,1)} %copy-done.6), custom_call_target="tpu_custom_call" | custom-call | flops 167772160 | bytes 1966080 | tf_op jit(solution)/shard_map/relay/pallas_call | solution.py:78
  45.0 5.7 %all-to-all-start = ((bf16[8,32,2560]{2,1,0:T(8,128)(2,1)}), bf16[8,32,2560]{2,1,0:T(8,128)(2,1)}, u32[]{:S(2)}, u32[]{:S(2)}) async-start(bf16[8,32,2560]{2,1,0:T(8,128)(2,1)} %bitcast.72), calls=%async_computation | async-start | bytes 2621440 | tf_op jit(solution)/shard_map/all_to_all | solution.py:266
  50.7 1.8 %collective-permute-start.11 = (bf16[32,1280]{1,0:T(8,128)(2,1)S(1)}, bf16[32,1280]{1,0:T(8,128)(2,1)S(1)}, u32[]{:S(2)}, u32[]{:S(2)}) collective-permute-start(bf16[32,1280]{1,0:T(8,128)(2,1)S(1)} %copy-done.24), channel_id=1, source_target_pairs={{0,16},{2,18},{4,20},{6,22},{8,24},{10,26},{12,28},{14,30},{16,0},... | collective-permute-start | bytes 245768 | tf_op jit(solution)/shard_map/ppermute | solution.py:221
  53.6 1.9 %collective-permute-start.13 = (bf16[32,1280]{1,0:T(8,128)(2,1)S(1)}, bf16[32,1280]{1,0:T(8,128)(2,1)S(1)}, u32[]{:S(2)}, u32[]{:S(2)}) collective-permute-start(bf16[32,1280]{1,0:T(8,128)(2,1)S(1)} %copy-done.22), channel_id=1, source_target_pairs={{0,20},{2,22},{4,16},{6,18},{8,28},{10,30},{12,24},{14,26},{16,4},... | collective-permute-start | bytes 245768 | tf_op jit(solution)/shard_map/ppermute | solution.py:221
  55.5 1.4 collective-permute-start.14
  56.9 1.3 collective-permute-start
  58.2 11.0 %collective-permute-done.11.refs_8_ = bf16[32,1280]{1,0:T(8,128)(2,1)S(1)} collective-permute-done((bf16[32,1280]{1,0:T(8,128)(2,1)S(1)}, bf16[32,1280]{1,0:T(8,128)(2,1)S(1)}, u32[]{:S(2)}, u32[]{:S(2)}) %collective-permute-start.11) | collective-permute-done | bytes 81952 | tf_op jit(solution)/shard_map/ppermute | solution.py:221
  69.2 2.6 %collective-permute-done.12.refs_9_ = bf16[32,1280]{1,0:T(8,128)(2,1)S(1)} collective-permute-done((bf16[32,1280]{1,0:T(8,128)(2,1)S(1)}, bf16[32,1280]{1,0:T(8,128)(2,1)S(1)}, u32[]{:S(2)}, u32[]{:S(2)}) %collective-permute-start.12) | collective-permute-done | bytes 81952 | tf_op jit(solution)/shard_map/ppermute | solution.py:221
  73.3 1.2 collective-permute-start.2
  76.1 1.2 collective-permute-start.3
  77.3 1.3 collective-permute-done.15.refs_12_
  79.2 5.9 %collective-permute-done.16.refs_13_ = bf16[32,1280]{1,0:T(8,128)(2,1)S(1)} collective-permute-done((bf16[32,1280]{1,0:T(8,128)(2,1)S(1)}, bf16[32,1280]{1,0:T(8,128)(2,1)S(1)}, u32[]{:S(2)}, u32[]{:S(2)}) %collective-permute-start.16) | collective-permute-done | bytes 81952 | tf_op jit(solution)/shard_map/ppermute | solution.py:221
  85.7 6.0 %collective-permute-done.17.refs_14_ = bf16[32,1280]{1,0:T(8,128)(2,1)S(1)} collective-permute-done((bf16[32,1280]{1,0:T(8,128)(2,1)}, bf16[32,1280]{1,0:T(8,128)(2,1)S(1)}, u32[]{:S(2)}, u32[]{:S(2)}) %collective-permute-start.17) | collective-permute-done | bytes 81952 | tf_op jit(solution)/shard_map/ppermute | solution.py:221
  93.3 2.1 %fusion.12.spread_ref = bf16[512,512]{1,0:T(8,128)(2,1)} fusion(s32[2,512]{1,0:T(2,128)S(1)} %get-tuple-element.48, s32[2,512]{1,0:T(2,128)S(1)} %get-tuple-element.49, s32[2,512]{1,0:T(2,128)} %get-tuple-element.50, s32[512]{0:T(512)} %bitcast.78, s32[2,512]{1,0:T(2,128)} %get-tuple-element.51, bf16[512]{0:T(512)(128)(2,1)S(1)} %get-tuple-element.39, ...), kind=kLoop, calls=%fused_computation.16 | loop fusion | flops 2883584 | bytes 546816 | tf_op jit(solution)/shard_map/add | solution.py:255
  95.4 3.4 %collective-permute-done.18.refs_15_ = bf16[32,1280]{1,0:T(8,128)(2,1)S(1)} collective-permute-done((bf16[32,1280]{1,0:T(8,128)(2,1)}, bf16[32,1280]{1,0:T(8,128)(2,1)S(1)}, u32[]{:S(2)}, u32[]{:S(2)}) %collective-permute-start.18) | collective-permute-done | bytes 81952 | tf_op jit(solution)/shard_map/ppermute | solution.py:221
  99.5 2.0 %collective-permute-start.5 = (bf16[32,3840]{1,0:T(8,128)(2,1)}, bf16[32,3840]{1,0:T(8,128)(2,1)}, u32[]{:S(2)}, u32[]{:S(2)}) collective-permute-start(bf16[32,3840]{1,0:T(8,128)(2,1)} %get-tuple-element.25), channel_id=1, source_target_pairs={{0,10},{2,8},{4,14},{6,12},{8,2},{10,0},{12,6},{14,4},{16,26},{18,... | collective-permute-start | bytes 737288 | tf_op jit(solution)/shard_map/ppermute | solution.py:221
  101.5 2.3 %collective-permute-start.7 = (bf16[32,3840]{1,0:T(8,128)(2,1)}, bf16[32,3840]{1,0:T(8,128)(2,1)}, u32[]{:S(2)}, u32[]{:S(2)}) collective-permute-start(bf16[32,3840]{1,0:T(8,128)(2,1)} %get-tuple-element.27), channel_id=1, source_target_pairs={{0,14},{2,12},{4,10},{6,8},{8,6},{10,4},{12,2},{14,0},{16,30},{18,... | collective-permute-start | bytes 737288 | tf_op jit(solution)/shard_map/ppermute | solution.py:221
  103.9 3.5 %fusion.18 = f32[40,137,128]{2,0,1:T(8,128)} fusion(bf16[40,137,128]{2,0,1:T(8,128)(2,1)} %param.10, bf16[1,80,80]{2,1,0:T(8,128)(2,1)S(1)} %copy-done.16, s32[]{:T(128)S(6)} %select_n.47, s32[]{:T(128)S(6)} %select_n.49), kind=kOutput, calls=%fused_computation.29 | convolution fusion | flops 56115200 | bytes 4218888 | tf_op jit(solution)/shard_map/klc,km->mlc/dot_general | solution.py:19
  107.4 6.1 %collective-permute-done.5.refs_5_ = bf16[32,3840]{1,0:T(8,128)(2,1)} collective-permute-done((bf16[32,3840]{1,0:T(8,128)(2,1)}, bf16[32,3840]{1,0:T(8,128)(2,1)}, u32[]{:S(2)}, u32[]{:S(2)}) %collective-permute-start.5) | collective-permute-done | bytes 245792 | tf_op jit(solution)/shard_map/ppermute | solution.py:221
  113.6 3.8 %collective-permute-done.6.refs_6_ = bf16[32,3840]{1,0:T(8,128)(2,1)} collective-permute-done((bf16[32,3840]{1,0:T(8,128)(2,1)}, bf16[32,3840]{1,0:T(8,128)(2,1)}, u32[]{:S(2)}, u32[]{:S(2)}) %collective-permute-start.6) | collective-permute-done | bytes 245792 | tf_op jit(solution)/shard_map/ppermute | solution.py:221
  117.4 5.8 %collective-permute-done.7.refs_7_ = bf16[32,3840]{1,0:T(8,128)(2,1)} collective-permute-done((bf16[32,3840]{1,0:T(8,128)(2,1)}, bf16[32,3840]{1,0:T(8,128)(2,1)}, u32[]{:S(2)}, u32[]{:S(2)}) %collective-permute-start.7) | collective-permute-done | bytes 245792 | tf_op jit(solution)/shard_map/ppermute | solution.py:221
  123.3 3.6 %prior.2.refs_9_ = f32[96,40,512]{2,1,0:T(8,128)} custom-call(f32[96]{0:T(128)} %bias_ref.3, s32[1]{0:T(128)} %bitcast.4.place_ref, bf16[512,512]{1,0:T(8,128)(2,1)} %fusion.12.spread_ref, bf16[32,3840]{1,0:T(8,128)(2,1)} %get-tuple-element.20.refs_0_, bf16[32,3840]{1,0:T(8,128)(2,1)} %copy-done.2, bf16[32,3840]{1,0:T(8,128)(2,1)} %copy-done.3, ...), custom_call_target="tpu_custom_call" | custom-call | flops 671088640 | bytes 3932160 | tf_op jit(solution)/shard_map/prior/pallas_call | solution.py:148
  126.8 4.0 %add_convert_fusion = bf16[40,137,128]{2,0,1:T(8,128)(2,1)} fusion(f32[40,137,128]{2,0,1:T(8,128)} %fusion.18, bf16[40,137,128]{2,0,1:T(8,128)(2,1)} %collective-permute-done, f32[137,128]{1,0:T(8,128)S(1)} %convert_element_type.16, bf16[1,80,80]{2,1,0:T(8,128)(2,1)S(1)} %copy-done.16, s32[]{:T(128)S(6)} %select_n.51, s32[]{:T(128)S(6)} %select_n.49), kind=kOutput, calls=%fused_computation.2 | convolution fusion | flops 58219520 | bytes 5695496 | tf_op jit(solution)/shard_map/klc,km->mlc/dot_general | solution.py:19
  130.8 5.0 %prior.3 = f32[96,40,512]{2,1,0:T(8,128)} custom-call(f32[96]{0:T(128)} %bias_ref.3, s32[1]{0:T(128)} %bitcast.4.place_ref, bf16[512,512]{1,0:T(8,128)(2,1)} %fusion.12.spread_ref, bf16[32,3840]{1,0:T(8,128)(2,1)} %get-tuple-element.20.refs_0_, bf16[32,3840]{1,0:T(8,128)(2,1)} %copy-done.2, ...), custom_call_target="tpu_custom_call", output_to_operand_aliasing={{}: (12, {})} | custom-call | flops 1342177280 | bytes 7864320 | tf_op jit(solution)/shard_map/prior/pallas_call | solution.py:148
  (80 shorter events, 10.4 us)
Async XLA Ops:
  5.8 8.3 %copy-start.17 = (s32[1,16,32]{2,1,0:T(8,128)S(1)}, s32[1,16,32]{2,1,0:T(8,128)}, u32[]{:S(2)}) copy-start(s32[1,16,32]{2,1,0:T(8,128)} %param.16) | copy-start | bytes 6148
  8.9 31.9 %collective-permute-start.10 = (bf16[128,1280]{1,0:T(8,128)(2,1)}, bf16[128,1280]{1,0:T(8,128)(2,1)S(1)}, u32[]{:S(2)}, u32[]{:S(2)}) collective-permute-start(bf16[128,1280]{1,0:T(8,128)(2,1)} %get-tuple-element.29), channel_id=1, source_target_pairs={{0,16},{2,18},{4,20},{6,22},{8,24},{10,26},{12,28},{14,30},{16,0},... | collective-permute-start | bytes 983048 | tf_op jit(solution)/shard_map/ppermute | solution.py:246
  14.1 26.7 %collective-permute-start.9 = (bf16[128,1280]{1,0:T(8,128)(2,1)}, bf16[128,1280]{1,0:T(8,128)(2,1)S(1)}, u32[]{:S(2)}, u32[]{:S(2)}) collective-permute-start(bf16[128,1280]{1,0:T(8,128)(2,1)} %get-tuple-element.28), channel_id=1, source_target_pairs={{0,16},{2,18},{4,20},{6,22},{8,24},{10,26},{12,28},{14,30},{16,0},... | collective-permute-start | bytes 983048 | tf_op jit(solution)/shard_map/ppermute | solution.py:246
  14.1 25.8 %collective-permute-start.8 = (s32[8,32]{1,0:T(8,128)S(1)}, s32[8,32]{1,0:T(8,128)S(1)}, u32[]{:S(2)}, u32[]{:S(2)}) collective-permute-start(s32[8,32]{1,0:T(8,128)S(1)} %dynamic-slice_bitcast_fusion), channel_id=1, source_target_pairs={{0,16},{2,18},{4,20},{6,22},{8,24},{10,26},{12,28},{14,30},{16,0},... | collective-permute-start | bytes 3080 | tf_op jit(solution)/shard_map/ppermute | solution.py:211
  44.9 7.6 %copy-start.23 = (bf16[32,1280]{1,0:T(8,128)(2,1)S(1)}, bf16[32,1280]{1,0:T(8,128)(2,1)}, u32[]{:S(2)}) copy-start(bf16[32,1280]{1,0:T(8,128)(2,1)} %get-tuple-element.31) | copy-start | bytes 245764
  44.9 8.7 %copy-start.22 = (bf16[32,1280]{1,0:T(8,128)(2,1)S(1)}, bf16[32,1280]{1,0:T(8,128)(2,1)}, u32[]{:S(2)}) copy-start(bf16[32,1280]{1,0:T(8,128)(2,1)} %get-tuple-element.32) | copy-start | bytes 245764
  44.9 10.6 %copy-start.21 = (bf16[32,1280]{1,0:T(8,128)(2,1)S(1)}, bf16[32,1280]{1,0:T(8,128)(2,1)}, u32[]{:S(2)}) copy-start(bf16[32,1280]{1,0:T(8,128)(2,1)} %get-tuple-element.33) | copy-start | bytes 245764
  44.9 13.2 %copy-start.18 = (s32[512,4]{0,1:T(4,128)S(1)}, s32[512,4]{0,1:T(4,128)}, u32[]{:S(2)}) copy-start(s32[512,4]{0,1:T(4,128)} %param.17) | copy-start | bytes 24580
  44.9 24.3 %copy-start.20 = (bf16[32,1280]{1,0:T(8,128)(2,1)S(1)}, bf16[32,1280]{1,0:T(8,128)(2,1)}, u32[]{:S(2)}) copy-start(bf16[32,1280]{1,0:T(8,128)(2,1)} %get-tuple-element.34) | copy-start | bytes 245764
  44.9 33.6 %copy-start.19 = (bf16[32,1280]{1,0:T(8,128)(2,1)S(1)}, bf16[32,1280]{1,0:T(8,128)(2,1)}, u32[]{:S(2)}) copy-start(bf16[32,1280]{1,0:T(8,128)(2,1)} %get-tuple-element.35) | copy-start | bytes 245764
  44.9 40.8 %copy-start.15 = (bf16[137,128]{1,0:T(8,128)(2,1)S(1)}, bf16[137,128]{1,0:T(8,128)(2,1)}, u32[]{:S(2)}) copy-start(bf16[137,128]{1,0:T(8,128)(2,1)} %param.12) | copy-start | bytes 105220
  44.9 58.9 %copy-start.16 = (bf16[1,80,80]{2,1,0:T(8,128)(2,1)S(1)}, bf16[1,80,80]{2,1,0:T(8,128)(2,1)}, u32[]{:S(2)}) copy-start(bf16[1,80,80]{2,1,0:T(8,128)(2,1)} %param.11) | copy-start | bytes 38404
  45.0 85.9 %all-to-all-start = ((bf16[8,32,2560]{2,1,0:T(8,128)(2,1)}), bf16[8,32,2560]{2,1,0:T(8,128)(2,1)}, u32[]{:S(2)}, u32[]{:S(2)}) async-start(bf16[8,32,2560]{2,1,0:T(8,128)(2,1)} %bitcast.72), calls=%async_computation | async-start | bytes 2621440 | tf_op jit(solution)/shard_map/all_to_all | solution.py:266
  50.7 18.5 %collective-permute-start.11 = (bf16[32,1280]{1,0:T(8,128)(2,1)S(1)}, bf16[32,1280]{1,0:T(8,128)(2,1)S(1)}, u32[]{:S(2)}, u32[]{:S(2)}) collective-permute-start(bf16[32,1280]{1,0:T(8,128)(2,1)S(1)} %copy-done.24), channel_id=1, source_target_pairs={{0,16},{2,18},{4,20},{6,22},{8,24},{10,26},{12,28},{14,30},{16,0},... | collective-permute-start | bytes 245768 | tf_op jit(solution)/shard_map/ppermute | solution.py:221
  52.5 19.3 %collective-permute-start.12 = (bf16[32,1280]{1,0:T(8,128)(2,1)S(1)}, bf16[32,1280]{1,0:T(8,128)(2,1)S(1)}, u32[]{:S(2)}, u32[]{:S(2)}) collective-permute-start(bf16[32,1280]{1,0:T(8,128)(2,1)S(1)} %copy-done.23), channel_id=1, source_target_pairs={{0,18},{2,16},{4,22},{6,20},{8,26},{10,24},{12,30},{14,28},{16,2},... | collective-permute-start | bytes 245768 | tf_op jit(solution)/shard_map/ppermute | solution.py:221
  53.6 19.1 %collective-permute-start.13 = (bf16[32,1280]{1,0:T(8,128)(2,1)S(1)}, bf16[32,1280]{1,0:T(8,128)(2,1)S(1)}, u32[]{:S(2)}, u32[]{:S(2)}) collective-permute-start(bf16[32,1280]{1,0:T(8,128)(2,1)S(1)} %copy-done.22), channel_id=1, source_target_pairs={{0,20},{2,22},{4,16},{6,18},{8,28},{10,30},{12,24},{14,26},{16,4},... | collective-permute-start | bytes 245768 | tf_op jit(solution)/shard_map/ppermute | solution.py:221
  55.5 19.9 %collective-permute-start.14 = (bf16[32,1280]{1,0:T(8,128)(2,1)S(1)}, bf16[32,1280]{1,0:T(8,128)(2,1)S(1)}, u32[]{:S(2)}, u32[]{:S(2)}) collective-permute-start(bf16[32,1280]{1,0:T(8,128)(2,1)S(1)} %copy-done.21), channel_id=1, source_target_pairs={{0,22},{2,20},{4,18},{6,16},{8,30},{10,28},{12,26},{14,24},{16,6},... | collective-permute-start | bytes 245768 | tf_op jit(solution)/shard_map/ppermute | solution.py:221
  56.9 70.0 %collective-permute-start = (bf16[40,137,128]{2,0,1:T(8,128)(2,1)}, bf16[40,137,128]{2,0,1:T(8,128)(2,1)}, u32[]{:S(2)}, u32[]{:S(2)}) collective-permute-start(bf16[40,137,128]{2,0,1:T(8,128)(2,1)} %param.10), channel_id=1, source_target_pairs={{1,0},{0,1},{3,2},{2,3},{5,4},{4,5},{7,6},{6,7},{9,8},{8,9},{11,10... | collective-permute-start | bytes 4208648 | tf_op jit(solution)/shard_map/ppermute | solution.py:282
  69.2 9.4 %collective-permute-start.15 = (bf16[32,1280]{1,0:T(8,128)(2,1)S(1)}, bf16[32,1280]{1,0:T(8,128)(2,1)}, u32[]{:S(2)}, u32[]{:S(2)}) collective-permute-start(bf16[32,1280]{1,0:T(8,128)(2,1)S(1)} %copy-done.20), channel_id=1, source_target_pairs={{0,24},{2,26},{4,28},{6,30},{8,16},{10,18},{12,20},{14,22},{16,8},... | collective-permute-start | bytes 245768 | tf_op jit(solution)/shard_map/ppermute | solution.py:221
  72.5 27.0 %collective-permute-start.1 = (bf16[32,3840]{1,0:T(8,128)(2,1)}, bf16[32,3840]{1,0:T(8,128)(2,1)S(1)}, u32[]{:S(2)}, u32[]{:S(2)}) collective-permute-start(bf16[32,3840]{1,0:T(8,128)(2,1)} %get-tuple-element.21), channel_id=1, source_target_pairs={{0,2},{2,0},{4,6},{6,4},{8,10},{10,8},{12,14},{14,12},{16,18},{18,... | collective-permute-start | bytes 737288 | tf_op jit(solution)/shard_map/ppermute | solution.py:221
  73.3 28.2 %collective-permute-start.2 = (bf16[32,3840]{1,0:T(8,128)(2,1)}, bf16[32,3840]{1,0:T(8,128)(2,1)S(1)}, u32[]{:S(2)}, u32[]{:S(2)}) collective-permute-start(bf16[32,3840]{1,0:T(8,128)(2,1)} %get-tuple-element.22), channel_id=1, source_target_pairs={{0,4},{2,6},{4,0},{6,2},{8,12},{10,14},{12,8},{14,10},{16,20},{18,... | collective-permute-start | bytes 737288 | tf_op jit(solution)/shard_map/ppermute | solution.py:221
  76.1 25.5 %collective-permute-start.3 = (bf16[32,3840]{1,0:T(8,128)(2,1)}, bf16[32,3840]{1,0:T(8,128)(2,1)S(1)}, u32[]{:S(2)}, u32[]{:S(2)}) collective-permute-start(bf16[32,3840]{1,0:T(8,128)(2,1)} %get-tuple-element.23), channel_id=1, source_target_pairs={{0,6},{2,4},{4,2},{6,0},{8,14},{10,12},{12,10},{14,8},{16,22},{18,... | collective-permute-start | bytes 737288 | tf_op jit(solution)/shard_map/ppermute | solution.py:221
  78.6 6.5 %collective-permute-start.16 = (bf16[32,1280]{1,0:T(8,128)(2,1)S(1)}, bf16[32,1280]{1,0:T(8,128)(2,1)S(1)}, u32[]{:S(2)}, u32[]{:S(2)}) collective-permute-start(bf16[32,1280]{1,0:T(8,128)(2,1)S(1)} %copy-done.19), channel_id=1, source_target_pairs={{0,26},{2,24},{4,30},{6,28},{8,18},{10,16},{12,22},{14,20},{16,10}... | collective-permute-start | bytes 245768 | tf_op jit(solution)/shard_map/ppermute | solution.py:221
  85.1 13.8 %copy-start.12 = (bf16[32,1280]{1,0:T(8,128)(2,1)}, bf16[32,1280]{1,0:T(8,128)(2,1)S(1)}, u32[]{:S(2)}) copy-start(bf16[32,1280]{1,0:T(8,128)(2,1)S(1)} %collective-permute-done.16.refs_13_) | copy-start | bytes 245764
  85.1 6.7 %collective-permute-start.17 = (bf16[32,1280]{1,0:T(8,128)(2,1)}, bf16[32,1280]{1,0:T(8,128)(2,1)S(1)}, u32[]{:S(2)}, u32[]{:S(2)}) collective-permute-start(bf16[32,1280]{1,0:T(8,128)(2,1)} %get-tuple-element.36), channel_id=1, source_target_pairs={{0,28},{2,30},{4,24},{6,26},{8,20},{10,22},{12,16},{14,18},{16,12}... | collective-permute-start | bytes 245768 | tf_op jit(solution)/shard_map/ppermute | solution.py:221
  91.7 7.1 %collective-permute-start.18 = (bf16[32,1280]{1,0:T(8,128)(2,1)}, bf16[32,1280]{1,0:T(8,128)(2,1)S(1)}, u32[]{:S(2)}, u32[]{:S(2)}) collective-permute-start(bf16[32,1280]{1,0:T(8,128)(2,1)} %get-tuple-element.37), channel_id=1, source_target_pairs={{0,30},{2,28},{4,26},{6,24},{8,22},{10,20},{12,18},{14,16},{16,14}... | collective-permute-start | bytes 245768 | tf_op jit(solution)/shard_map/ppermute | solution.py:221
  99.5 8.0 %collective-permute-start.4 = (bf16[32,3840]{1,0:T(8,128)(2,1)}, bf16[32,3840]{1,0:T(8,128)(2,1)S(1)}, u32[]{:S(2)}, u32[]{:S(2)}) collective-permute-start(bf16[32,3840]{1,0:T(8,128)(2,1)} %get-tuple-element.24), channel_id=1, source_target_pairs={{0,8},{2,10},{4,12},{6,14},{8,0},{10,2},{12,4},{14,6},{16,24},{18,... | collective-permute-start | bytes 737288 | tf_op jit(solution)/shard_map/ppermute | solution.py:221
  99.5 7.9 %copy-start.2 = (bf16[32,3840]{1,0:T(8,128)(2,1)}, bf16[32,3840]{1,0:T(8,128)(2,1)S(1)}, u32[]{:S(2)}) copy-start(bf16[32,3840]{1,0:T(8,128)(2,1)S(1)} %collective-permute-done.1.refs_1_) | copy-start | bytes 737284
  99.5 14.1 %collective-permute-start.5 = (bf16[32,3840]{1,0:T(8,128)(2,1)}, bf16[32,3840]{1,0:T(8,128)(2,1)}, u32[]{:S(2)}, u32[]{:S(2)}) collective-permute-start(bf16[32,3840]{1,0:T(8,128)(2,1)} %get-tuple-element.25), channel_id=1, source_target_pairs={{0,10},{2,8},{4,14},{6,12},{8,2},{10,0},{12,6},{14,4},{16,26},{18,... | collective-permute-start | bytes 737288 | tf_op jit(solution)/shard_map/ppermute | solution.py:221
  101.5 15.9 %collective-permute-start.6 = (bf16[32,3840]{1,0:T(8,128)(2,1)}, bf16[32,3840]{1,0:T(8,128)(2,1)}, u32[]{:S(2)}, u32[]{:S(2)}) collective-permute-start(bf16[32,3840]{1,0:T(8,128)(2,1)} %get-tuple-element.26), channel_id=1, source_target_pairs={{0,12},{2,14},{4,8},{6,10},{8,4},{10,6},{12,0},{14,2},{16,28},{18,... | collective-permute-start | bytes 737288 | tf_op jit(solution)/shard_map/ppermute | solution.py:221
  101.5 21.7 %collective-permute-start.7 = (bf16[32,3840]{1,0:T(8,128)(2,1)}, bf16[32,3840]{1,0:T(8,128)(2,1)}, u32[]{:S(2)}, u32[]{:S(2)}) collective-permute-start(bf16[32,3840]{1,0:T(8,128)(2,1)} %get-tuple-element.27), channel_id=1, source_target_pairs={{0,14},{2,12},{4,10},{6,8},{8,6},{10,4},{12,2},{14,0},{16,30},{18,... | collective-permute-start | bytes 737288 | tf_op jit(solution)/shard_map/ppermute | solution.py:221
  107.4 15.8 %copy-start.5 = (bf16[32,3840]{1,0:T(8,128)(2,1)}, bf16[32,3840]{1,0:T(8,128)(2,1)S(1)}, u32[]{:S(2)}) copy-start(bf16[32,3840]{1,0:T(8,128)(2,1)S(1)} %collective-permute-done.4.refs_4_) | copy-start | bytes 737284
  (13 other events, 34.6 us)
where the time goes:
time: 138 us; the launch traced here: 136 us
  waiting for transfers between devices  70.8 us (51%)
  starting transfers between devices  25.3 us (18%)
  Pallas kernels  17.1 us (12%)
  matrix products  9.63 us (7%)
  local copies, waits for them, and re-layouts  9.21 us (7%)
  other arithmetic  2.85 us (2%)
    ppermute x15, waiting for transfers between devices, to_partner(): return lax.ppermute(array, 'tile', [(i, i ^ d) for i in range(n_tile)])  47.3 us
    ppermute x1, waiting for transfers between devices, shards(): relay_cols = lax.ppermute(far_cols, 'tile', mirror)  23.5 us
    ppermute x15, starting transfers between devices, to_partner(): return lax.ppermute(array, 'tile', [(i, i ^ d) for i in range(n_tile)])  13.6 us
    dot_general x4, matrix products, dot(): return jnp.einsum(spec, a, b, preferred_element_type=jnp.float32)  9.63 us
    pallas_call x2, Pallas kernels, prior_piece(): pl.pallas_call(functools.partial(prior_kernel, first, count, block, mem_d...  8.53 us
    unnamed x54, local copies, waits for them, and re-layouts  6.94 us
    pallas_call x2, Pallas kernels, pack(): pl.pallas_call(functools.partial(pack_kernel, sends, relays), in_specs=[p...  5.95 us
    all_to_all x1, starting transfers between devices, shards(): lax.all_to_all(relayed, 'tile', 0, 0, tiled=True, axis_index_groups=halves)  5.71 us
  transfers between devices with their start and end apart: 20, of which 12 were waited for; matrix products, arithmetic and copies ran while one was open for 9% of the time, Pallas kernels for 5%

commit v1 on v0

--- a/solution.py
+++ b/solution.py
@@ -90,7 +90,18 @@
 def prior_kernel(
     first, count, block, mem_dev, sources, bias_ref, place_ref, spread_ref, *refs
 ):
-    prior_ref, table_ref, done_ref, sems = refs[-4:]
+    prior_ref, table_ref, done_ref, sems, far_ref, far_sems = refs[-6:]
+    width = block * mem_dev
+    spans = [slice(i * width, (i + 1) * width) for i in range(count)]
+    near_refs, far_refs, loads = refs[: sources[0]], refs[sources[0] : sum(sources)], []
+    if sources[1] == 1:
+        for i, span in enumerate(spans):
+            at = (slice(None), span)
+            loads.append(
+                pltpu.make_async_copy(far_refs[0].at[at], far_ref.at[at], far_sems.at[i])
+            )
+            loads[-1].start()
+        far_refs = (far_ref,)
 
     start = 0
     for side in range(2):
@@ -102,11 +113,11 @@
             table_ref[start : start + rows] = spread_ref[pl.ds(at, rows)]
             start += rows
 
-    width = block * mem_dev
     copies = []
-    for i in range(count):
-        lanes = slice(i * width, (i + 1) * width)
-        rows = jnp.concatenate([ref[:, lanes] for ref in refs[: sum(sources)]], axis=0)
+    for i, span in enumerate(spans):
+        if loads:
+            loads[i].wait()
+        rows = jnp.concatenate([ref[:, span] for ref in (*near_refs, *far_refs)], axis=0)
         total = lax.dot_general(
             rows,
             table_ref[...],
@@ -137,7 +148,7 @@
         pl.BlockSpec(memory_space=pltpu.SMEM),
         pl.BlockSpec(memory_space=pltpu.VMEM),
         *[pl.BlockSpec((slots, width), lambda i: (0, first // count))] * len(near),
-        *[pl.BlockSpec(memory_space=pltpu.VMEM)] * len(far),
+        *[pl.BlockSpec(memory_space=pl.ANY if len(far) == 1 else pltpu.VMEM)] * len(far),
     ]
     operands = [bias, place, spread, *near, *far]
     aliases = {}
@@ -156,6 +167,8 @@
         scratch_shapes=[
             pltpu.VMEM(spread.shape, spread.dtype),
             pltpu.VMEM((count, block, mem_dev, obs_count), jnp.float32),
+            pltpu.SemaphoreType.DMA((count,)),
+            pltpu.VMEM(far[0].shape, far[0].dtype),
             pltpu.SemaphoreType.DMA((count,)),
         ],
         input_output_aliases=aliases,
@@ -230,13 +243,13 @@
     late = [d for d in range(half) if d not in early]
     direct_to = range(half, n_tile) if direct else ()
     near = [None] * half
-    sent, seen = pack(*args, [(d, 0, total) for d in early], windows[:1])
+    sent, seen = pack(*args, [(d, 0, total) for d in early], windows[:-1])
     for d, array in zip(early, sent):
         near[d] = array
     sent, more = pack(
         *args,
         [(d, 0, total) for d in late] + [(d, *windows[-1]) for d in direct_to],
-        windows[1:-1],
+        [],
     )
     for d, array in zip(late, sent):
         near[d] = array
@@ -279,9 +292,7 @@
     for shift in range(n_mem):
         piece = anomalies
         if shift:
-            piece = lax.ppermute(
-                anomalies, "mem", [((i + shift) % n_mem, i) for i in range(n_mem)]
-            )
+            piece = lax.ppermute(anomalies, "mem", [((i + shift) % n_mem, i) for i in range(n_mem)])
         start = lax.rem(mine + shift, n_mem) * mem_dev
         part = lax.dynamic_slice_in_dim(weight_cols, start, mem_dev, 0)
         mixture = mixture + dot("klc,km->mlc", piece, part)

time: 138 us -> 139 us (level)
    ppermute x1, waiting for transfers between devices: 23.5 us -> 26.4 us  [shards(): relay_cols = lax.ppermute(far_cols, 'tile', mirror)]
    ppermute x15, waiting for transfers between devices: 47.3 us -> 44.7 us  [to_partner(): return lax.ppermute(array, 'tile', [(i, i ^ d) for i in range(n_tile)])]
    unnamed x54 -> x42, local copies, waits for them, and re-layouts: 6.94 us -> 6.92 us
where the time goes in v1:
time: 139 us; the launch traced here: 137 us
  waiting for transfers between devices  71.1 us (51%)
  starting transfers between devices  25.2 us (18%)
  Pallas kernels  17.8 us (13%)
  matrix products  9.61 us (7%)
  local copies, waits for them, and re-layouts  9.19 us (7%)
  other arithmetic  2.8 us (2%)
    ppermute x15, waiting for transfers between devices, to_partner(): return lax.ppermute(array, 'tile', [(i, i ^ d) for i in range(n_tile)])  44.7 us
    ppermute x1, waiting for transfers between devices, shards(): relay_cols = lax.ppermute(far_cols, 'tile', mirror)  26.4 us
    ppermute x15, starting transfers between devices, to_partner(): return lax.ppermute(array, 'tile', [(i, i ^ d) for i in range(n_tile)])  13.6 us
    dot_general x4, matrix products, dot(): return jnp.einsum(spec, a, b, preferred_element_type=jnp.float32)  9.61 us
    pallas_call x2, Pallas kernels, prior_piece(): pl.pallas_call(functools.partial(prior_kernel, first, count, block, mem_d...  9.38 us
    unnamed x42, local copies, waits for them, and re-layouts  6.92 us
    pallas_call x2, Pallas kernels, pack(): pl.pallas_call(functools.partial(pack_kernel, sends, relays), in_specs=[p...  5.71 us
    all_to_all x1, starting transfers between devices, shards(): lax.all_to_all(relayed, 'tile', 0, 0, tiled=True, axis_index_groups=halves)  5.69 us
  transfers between devices with their start and end apart: 20, of which 12 were waited for; matrix products, arithmetic and copies ran while one was open for 9% of the time, Pallas kernels for 5%

profile of v1, /device:TPU:11, one launch (start us, length us, event | category | flops | bytes accessed | tf_op | source)
XLA Modules:
  0.0 136.6 jit_solution(6901748718837376145)
XLA Ops:
  0.7 1.7 %copy-done = bf16[8461,137]{0,1:T(8,128)(2,1)S(1)} copy-done((bf16[8461,137]{0,1:T(8,128)(2,1)S(1)}, bf16[8461,137]{0,1:T(8,128)(2,1)}, u32[]{:S(2)}) %copy-start) | copy-done | bytes 2318338
  2.3 1.6 %fusion.7 = bf16[96,137]{0,1:T(8,128)(2,1)S(1)} fusion(bf16[8461,137]{0,1:T(8,128)(2,1)S(1)} %copy-done, s32[96]{0:T(128)} %param.15), kind=kOutput, calls=%fused_computation.7 | convolution fusion | flops 223383552 | bytes 2345002 | tf_op jit(solution)/shard_map/cs,sl->cl/dot_general | solution.py:19
  4.5 1.3 copy.16
  5.8 2.8 %pack.3 = (bf16[32,3840]{1,0:T(8,128)(2,1)}, bf16[32,3840]{1,0:T(8,128)(2,1)}, bf16[32,3840]{1,0:T(8,128)(2,1)}, bf16[32,3840]{1,0:T(8,128)(2,1)}, bf16[128,1280]{1,0:T(8,128)(2,1)}, /*index=5*/bf16[128,1280]{1,0:T(8,128)(2,1)}) custom-call(s32[1]{0:T(128)} %bitcast.14.me_ref, s32[16,32]{1,0:T(8,128)} %bitcast.75, bf16[3840,128]{1,0:T(8,128)(2,1)} %bitcast.73), custom_call_target="tpu_custom_call" | custom-call | flops 125829120 | bytes 2949120 | tf_op jit(solution)/shard_map/pack/pallas_call | solution.py:47
  8.6 2.3 %collective-permute-start.10 = (bf16[128,1280]{1,0:T(8,128)(2,1)}, bf16[128,1280]{1,0:T(8,128)(2,1)S(1)}, u32[]{:S(2)}, u32[]{:S(2)}) collective-permute-start(bf16[128,1280]{1,0:T(8,128)(2,1)} %get-tuple-element.29), channel_id=1, source_target_pairs={{0,16},{2,18},{4,20},{6,22},{8,24},{10,26},{12,28},{14,30},{16,0},... | collective-permute-start | bytes 983048 | tf_op jit(solution)/shard_map/ppermute | solution.py:259
  11.0 2.3 %collective-permute-start.8 = (s32[8,32]{1,0:T(8,128)S(1)}, s32[8,32]{1,0:T(8,128)S(1)}, u32[]{:S(2)}, u32[]{:S(2)}) collective-permute-start(s32[8,32]{1,0:T(8,128)S(1)} %dynamic-slice_bitcast_fusion), channel_id=1, source_target_pairs={{0,16},{2,18},{4,20},{6,22},{8,24},{10,26},{12,28},{14,30},{16,0},... | collective-permute-start | bytes 3080 | tf_op jit(solution)/shard_map/ppermute | solution.py:224
  13.3 26.4 %collective-permute-done.8 = s32[8,32]{1,0:T(8,128)S(1)} collective-permute-done((s32[8,32]{1,0:T(8,128)S(1)}, s32[8,32]{1,0:T(8,128)S(1)}, u32[]{:S(2)}, u32[]{:S(2)}) %collective-permute-start.8) | collective-permute-done | bytes 1056 | tf_op jit(solution)/shard_map/ppermute | solution.py:224
  42.0 2.7 %relay.1 = bf16[256,2560]{1,0:T(8,128)(2,1)} custom-call(bf16[256,128]{1,0:T(8,128)(2,1)} %fusion.15.hot_ref, bf16[128,1280]{1,0:T(8,128)(2,1)} %copy-done.7, bf16[128,1280]{1,0:T(8,128)(2,1)} %copy-done.6), custom_call_target="tpu_custom_call" | custom-call | flops 167772160 | bytes 1966080 | tf_op jit(solution)/shard_map/relay/pallas_call | solution.py:78
  44.7 5.7 %all-to-all-start = ((bf16[8,32,2560]{2,1,0:T(8,128)(2,1)}), bf16[8,32,2560]{2,1,0:T(8,128)(2,1)}, u32[]{:S(2)}, u32[]{:S(2)}) async-start(bf16[8,32,2560]{2,1,0:T(8,128)(2,1)} %bitcast.72), calls=%async_computation | async-start | bytes 2621440 | tf_op jit(solution)/shard_map/all_to_all | solution.py:279
  50.4 2.9 %pack.2 = (bf16[32,3840]{1,0:T(8,128)(2,1)}, bf16[32,3840]{1,0:T(8,128)(2,1)}, bf16[32,3840]{1,0:T(8,128)(2,1)}, bf16[32,3840]{1,0:T(8,128)(2,1)}, bf16[32,1280]...) custom-call(s32[1]{0:T(128)} %bitcast.14.me_ref, ...), custom_call_target="tpu_custom_call" | custom-call | flops 377487360 | bytes 4915200 | tf_op jit(solution)/shard_map/pack/pallas_call | solution.py:47
  53.3 1.8 %collective-permute-start.11 = (bf16[32,1280]{1,0:T(8,128)(2,1)}, bf16[32,1280]{1,0:T(8,128)(2,1)S(1)}, u32[]{:S(2)}, u32[]{:S(2)}) collective-permute-start(bf16[32,1280]{1,0:T(8,128)(2,1)} %get-tuple-element.30), channel_id=1, source_target_pairs={{0,16},{2,18},{4,20},{6,22},{8,24},{10,26},{12,28},{14,30},{16,0},... | collective-permute-start | bytes 245768 | tf_op jit(solution)/shard_map/ppermute | solution.py:234
  56.2 1.8 %collective-permute-start.13 = (bf16[32,1280]{1,0:T(8,128)(2,1)}, bf16[32,1280]{1,0:T(8,128)(2,1)S(1)}, u32[]{:S(2)}, u32[]{:S(2)}) collective-permute-start(bf16[32,1280]{1,0:T(8,128)(2,1)} %get-tuple-element.32), channel_id=1, source_target_pairs={{0,20},{2,22},{4,16},{6,18},{8,28},{10,30},{12,24},{14,26},{16,4},... | collective-permute-start | bytes 245768 | tf_op jit(solution)/shard_map/ppermute | solution.py:234
  58.1 1.4 %collective-permute-start.14 = (bf16[32,1280]{1,0:T(8,128)(2,1)}, bf16[32,1280]{1,0:T(8,128)(2,1)S(1)}, u32[]{:S(2)}, u32[]{:S(2)}) collective-permute-start(bf16[32,1280]{1,0:T(8,128)(2,1)} %get-tuple-element.33), channel_id=1, source_target_pairs={{0,22},{2,20},{4,18},{6,16},{8,30},{10,28},{12,26},{14,24},{16,6},... | collective-permute-start | bytes 245768 | tf_op jit(solution)/shard_map/ppermute | solution.py:234
  59.5 1.3 collective-permute-start
  60.8 8.1 %collective-permute-done.11.refs_8_ = bf16[32,1280]{1,0:T(8,128)(2,1)S(1)} collective-permute-done((bf16[32,1280]{1,0:T(8,128)(2,1)}, bf16[32,1280]{1,0:T(8,128)(2,1)S(1)}, u32[]{:S(2)}, u32[]{:S(2)}) %collective-permute-start.11) | collective-permute-done | bytes 81952 | tf_op jit(solution)/shard_map/ppermute | solution.py:234
  68.9 2.6 %collective-permute-done.12.refs_9_ = bf16[32,1280]{1,0:T(8,128)(2,1)S(1)} collective-permute-done((bf16[32,1280]{1,0:T(8,128)(2,1)}, bf16[32,1280]{1,0:T(8,128)(2,1)S(1)}, u32[]{:S(2)}, u32[]{:S(2)}) %collective-permute-start.12) | collective-permute-done | bytes 81952 | tf_op jit(solution)/shard_map/ppermute | solution.py:234
  73.0 1.2 collective-permute-start.2
  75.7 1.2 collective-permute-start.3
  76.9 1.3 collective-permute-done.15.refs_12_
  78.9 6.1 %collective-permute-done.16.refs_13_ = bf16[32,1280]{1,0:T(8,128)(2,1)S(1)} collective-permute-done((bf16[32,1280]{1,0:T(8,128)(2,1)}, bf16[32,1280]{1,0:T(8,128)(2,1)S(1)}, u32[]{:S(2)}, u32[]{:S(2)}) %collective-permute-start.16) | collective-permute-done | bytes 81952 | tf_op jit(solution)/shard_map/ppermute | solution.py:234
  85.6 6.0 %collective-permute-done.17.refs_14_ = bf16[32,1280]{1,0:T(8,128)(2,1)S(1)} collective-permute-done((bf16[32,1280]{1,0:T(8,128)(2,1)}, bf16[32,1280]{1,0:T(8,128)(2,1)S(1)}, u32[]{:S(2)}, u32[]{:S(2)}) %collective-permute-start.17) | collective-permute-done | bytes 81952 | tf_op jit(solution)/shard_map/ppermute | solution.py:234
  93.1 2.1 %fusion.12.spread_ref = bf16[512,512]{1,0:T(8,128)(2,1)} fusion(s32[2,512]{1,0:T(2,128)S(1)} %get-tuple-element.48, s32[2,512]{1,0:T(2,128)S(1)} %get-tuple-element.49, s32[2,512]{1,0:T(2,128)} %get-tuple-element.50, s32[512]{0:T(512)} %bitcast.78, s32[2,512]{1,0:T(2,128)} %get-tuple-element.51, bf16[512]{0:T(512)(128)(2,1)S(1)} %get-tuple-element.39, ...), kind=kLoop, calls=%fused_computation.16 | loop fusion | flops 2883584 | bytes 546816 | tf_op jit(solution)/shard_map/add | solution.py:268
  95.2 3.6 %collective-permute-done.18.refs_15_ = bf16[32,1280]{1,0:T(8,128)(2,1)S(1)} collective-permute-done((bf16[32,1280]{1,0:T(8,128)(2,1)}, bf16[32,1280]{1,0:T(8,128)(2,1)S(1)}, u32[]{:S(2)}, u32[]{:S(2)}) %collective-permute-start.18) | collective-permute-done | bytes 81952 | tf_op jit(solution)/shard_map/ppermute | solution.py:234
  99.4 2.0 %collective-permute-start.5 = (bf16[32,3840]{1,0:T(8,128)(2,1)}, bf16[32,3840]{1,0:T(8,128)(2,1)}, u32[]{:S(2)}, u32[]{:S(2)}) collective-permute-start(bf16[32,3840]{1,0:T(8,128)(2,1)} %get-tuple-element.25), channel_id=1, source_target_pairs={{0,10},{2,8},{4,14},{6,12},{8,2},{10,0},{12,6},{14,4},{16,26},{18,... | collective-permute-start | bytes 737288 | tf_op jit(solution)/shard_map/ppermute | solution.py:234
  101.4 2.3 %collective-permute-start.7 = (bf16[32,3840]{1,0:T(8,128)(2,1)}, bf16[32,3840]{1,0:T(8,128)(2,1)}, u32[]{:S(2)}, u32[]{:S(2)}) collective-permute-start(bf16[32,3840]{1,0:T(8,128)(2,1)} %get-tuple-element.27), channel_id=1, source_target_pairs={{0,14},{2,12},{4,10},{6,8},{8,6},{10,4},{12,2},{14,0},{16,30},{18,... | collective-permute-start | bytes 737288 | tf_op jit(solution)/shard_map/ppermute | solution.py:234
  103.8 3.5 %fusion.18 = f32[40,137,128]{2,0,1:T(8,128)} fusion(bf16[40,137,128]{2,0,1:T(8,128)(2,1)} %param.10, bf16[1,80,80]{2,1,0:T(8,128)(2,1)S(1)} %copy-done.16, s32[]{:T(128)S(6)} %select_n.47, s32[]{:T(128)S(6)} %select_n.49), kind=kOutput, calls=%fused_computation.29 | convolution fusion | flops 56115200 | bytes 4218888 | tf_op jit(solution)/shard_map/klc,km->mlc/dot_general | solution.py:19
  107.3 6.2 %collective-permute-done.5.refs_5_ = bf16[32,3840]{1,0:T(8,128)(2,1)} collective-permute-done((bf16[32,3840]{1,0:T(8,128)(2,1)}, bf16[32,3840]{1,0:T(8,128)(2,1)}, u32[]{:S(2)}, u32[]{:S(2)}) %collective-permute-start.5) | collective-permute-done | bytes 245792 | tf_op jit(solution)/shard_map/ppermute | solution.py:234
  113.5 3.8 %collective-permute-done.6.refs_6_ = bf16[32,3840]{1,0:T(8,128)(2,1)} collective-permute-done((bf16[32,3840]{1,0:T(8,128)(2,1)}, bf16[32,3840]{1,0:T(8,128)(2,1)}, u32[]{:S(2)}, u32[]{:S(2)}) %collective-permute-start.6) | collective-permute-done | bytes 245792 | tf_op jit(solution)/shard_map/ppermute | solution.py:234
  117.3 5.8 %collective-permute-done.7.refs_7_ = bf16[32,3840]{1,0:T(8,128)(2,1)} collective-permute-done((bf16[32,3840]{1,0:T(8,128)(2,1)}, bf16[32,3840]{1,0:T(8,128)(2,1)}, u32[]{:S(2)}, u32[]{:S(2)}) %collective-permute-start.7) | collective-permute-done | bytes 245792 | tf_op jit(solution)/shard_map/ppermute | solution.py:234
  123.2 3.6 %prior.2.refs_9_ = f32[96,40,512]{2,1,0:T(8,128)} custom-call(f32[96]{0:T(128)} %bias_ref.3, s32[1]{0:T(128)} %bitcast.4.place_ref, bf16[512,512]{1,0:T(8,128)(2,1)} %fusion.12.spread_ref, bf16[32,3840]{1,0:T(8,128)(2,1)} %get-tuple-element.20.refs_0_, bf16[32,3840]{1,0:T(8,128)(2,1)} %copy-done.2, bf16[32,3840]{1,0:T(8,128)(2,1)} %copy-done.3, ...), custom_call_target="tpu_custom_call" | custom-call | flops 671088640 | bytes 3932160 | tf_op jit(solution)/shard_map/prior/pallas_call | solution.py:159
  126.8 4.0 %add_convert_fusion = bf16[40,137,128]{2,0,1:T(8,128)(2,1)} fusion(f32[40,137,128]{2,0,1:T(8,128)} %fusion.18, bf16[40,137,128]{2,0,1:T(8,128)(2,1)} %collective-permute-done, f32[137,128]{1,0:T(8,128)S(1)} %convert_element_type.16, bf16[1,80,80]{2,1,0:T(8,128)(2,1)S(1)} %copy-done.16, s32[]{:T(128)S(6)} %select_n.51, s32[]{:T(128)S(6)} %select_n.49), kind=kOutput, calls=%fused_computation.2 | convolution fusion | flops 58219520 | bytes 5695496 | tf_op jit(solution)/shard_map/klc,km->mlc/dot_general | solution.py:19
  130.8 5.8 %prior.3 = f32[96,40,512]{2,1,0:T(8,128)} custom-call(f32[96]{0:T(128)} %bias_ref.3, s32[1]{0:T(128)} %bitcast.4.place_ref, bf16[512,512]{1,0:T(8,128)(2,1)} %fusion.12.spread_ref, bf16[32,3840]{1,0:T(8,128)(2,1)} %get-tuple-element.20.refs_0_, bf16[32,3840]{1,0:T(8,128)(2,1)} %copy-done.2, ...), custom_call_target="tpu_custom_call", output_to_operand_aliasing={{}: (12, {})} | custom-call | flops 1342177280 | bytes 7864320 | tf_op jit(solution)/shard_map/prior/pallas_call | solution.py:159
  (68 shorter events, 10.3 us)
Async XLA Ops:
  0.6 1.7 %copy-start = (bf16[8461,137]{0,1:T(8,128)(2,1)S(1)}, bf16[8461,137]{0,1:T(8,128)(2,1)}, u32[]{:S(2)}) copy-start(bf16[8461,137]{0,1:T(8,128)(2,1)} %param.14) | copy-start | bytes 6954946
  4.5 6.5 %copy-start.17 = (s32[1,16,32]{2,1,0:T(8,128)S(1)}, s32[1,16,32]{2,1,0:T(8,128)}, u32[]{:S(2)}) copy-start(s32[1,16,32]{2,1,0:T(8,128)} %param.16) | copy-start | bytes 6148
  8.6 31.9 %collective-permute-start.10 = (bf16[128,1280]{1,0:T(8,128)(2,1)}, bf16[128,1280]{1,0:T(8,128)(2,1)S(1)}, u32[]{:S(2)}, u32[]{:S(2)}) collective-permute-start(bf16[128,1280]{1,0:T(8,128)(2,1)} %get-tuple-element.29), channel_id=1, source_target_pairs={{0,16},{2,18},{4,20},{6,22},{8,24},{10,26},{12,28},{14,30},{16,0},... | collective-permute-start | bytes 983048 | tf_op jit(solution)/shard_map/ppermute | solution.py:259
  10.9 29.6 %collective-permute-start.9 = (bf16[128,1280]{1,0:T(8,128)(2,1)}, bf16[128,1280]{1,0:T(8,128)(2,1)S(1)}, u32[]{:S(2)}, u32[]{:S(2)}) collective-permute-start(bf16[128,1280]{1,0:T(8,128)(2,1)} %get-tuple-element.28), channel_id=1, source_target_pairs={{0,16},{2,18},{4,20},{6,22},{8,24},{10,26},{12,28},{14,30},{16,0},... | collective-permute-start | bytes 983048 | tf_op jit(solution)/shard_map/ppermute | solution.py:259
  11.0 28.7 %collective-permute-start.8 = (s32[8,32]{1,0:T(8,128)S(1)}, s32[8,32]{1,0:T(8,128)S(1)}, u32[]{:S(2)}, u32[]{:S(2)}) collective-permute-start(s32[8,32]{1,0:T(8,128)S(1)} %dynamic-slice_bitcast_fusion), channel_id=1, source_target_pairs={{0,16},{2,18},{4,20},{6,22},{8,24},{10,26},{12,28},{14,30},{16,0},... | collective-permute-start | bytes 3080 | tf_op jit(solution)/shard_map/ppermute | solution.py:224
  44.7 16.1 %copy-start.18 = (s32[512,4]{0,1:T(4,128)S(1)}, s32[512,4]{0,1:T(4,128)}, u32[]{:S(2)}) copy-start(s32[512,4]{0,1:T(4,128)} %param.17) | copy-start | bytes 24580
  44.7 40.9 %copy-start.15 = (bf16[137,128]{1,0:T(8,128)(2,1)S(1)}, bf16[137,128]{1,0:T(8,128)(2,1)}, u32[]{:S(2)}) copy-start(bf16[137,128]{1,0:T(8,128)(2,1)} %param.12) | copy-start | bytes 105220
  44.7 86.1 %all-to-all-start = ((bf16[8,32,2560]{2,1,0:T(8,128)(2,1)}), bf16[8,32,2560]{2,1,0:T(8,128)(2,1)}, u32[]{:S(2)}, u32[]{:S(2)}) async-start(bf16[8,32,2560]{2,1,0:T(8,128)(2,1)} %bitcast.72), calls=%async_computation | async-start | bytes 2621440 | tf_op jit(solution)/shard_map/all_to_all | solution.py:279
  50.4 53.4 %copy-start.16 = (bf16[1,80,80]{2,1,0:T(8,128)(2,1)S(1)}, bf16[1,80,80]{2,1,0:T(8,128)(2,1)}, u32[]{:S(2)}) copy-start(bf16[1,80,80]{2,1,0:T(8,128)(2,1)} %param.11) | copy-start | bytes 38404
  53.3 15.6 %collective-permute-start.11 = (bf16[32,1280]{1,0:T(8,128)(2,1)}, bf16[32,1280]{1,0:T(8,128)(2,1)S(1)}, u32[]{:S(2)}, u32[]{:S(2)}) collective-permute-start(bf16[32,1280]{1,0:T(8,128)(2,1)} %get-tuple-element.30), channel_id=1, source_target_pairs={{0,16},{2,18},{4,20},{6,22},{8,24},{10,26},{12,28},{14,30},{16,0},... | collective-permute-start | bytes 245768 | tf_op jit(solution)/shard_map/ppermute | solution.py:234
  55.1 16.4 %collective-permute-start.12 = (bf16[32,1280]{1,0:T(8,128)(2,1)}, bf16[32,1280]{1,0:T(8,128)(2,1)S(1)}, u32[]{:S(2)}, u32[]{:S(2)}) collective-permute-start(bf16[32,1280]{1,0:T(8,128)(2,1)} %get-tuple-element.31), channel_id=1, source_target_pairs={{0,18},{2,16},{4,22},{6,20},{8,26},{10,24},{12,30},{14,28},{16,2},... | collective-permute-start | bytes 245768 | tf_op jit(solution)/shard_map/ppermute | solution.py:234
  56.2 16.2 %collective-permute-start.13 = (bf16[32,1280]{1,0:T(8,128)(2,1)}, bf16[32,1280]{1,0:T(8,128)(2,1)S(1)}, u32[]{:S(2)}, u32[]{:S(2)}) collective-permute-start(bf16[32,1280]{1,0:T(8,128)(2,1)} %get-tuple-element.32), channel_id=1, source_target_pairs={{0,20},{2,22},{4,16},{6,18},{8,28},{10,30},{12,24},{14,26},{16,4},... | collective-permute-start | bytes 245768 | tf_op jit(solution)/shard_map/ppermute | solution.py:234
  58.1 17.1 %collective-permute-start.14 = (bf16[32,1280]{1,0:T(8,128)(2,1)}, bf16[32,1280]{1,0:T(8,128)(2,1)S(1)}, u32[]{:S(2)}, u32[]{:S(2)}) collective-permute-start(bf16[32,1280]{1,0:T(8,128)(2,1)} %get-tuple-element.33), channel_id=1, source_target_pairs={{0,22},{2,20},{4,18},{6,16},{8,30},{10,28},{12,26},{14,24},{16,6},... | collective-permute-start | bytes 245768 | tf_op jit(solution)/shard_map/ppermute | solution.py:234
  59.5 67.3 %collective-permute-start = (bf16[40,137,128]{2,0,1:T(8,128)(2,1)}, bf16[40,137,128]{2,0,1:T(8,128)(2,1)}, u32[]{:S(2)}, u32[]{:S(2)}) collective-permute-start(bf16[40,137,128]{2,0,1:T(8,128)(2,1)} %param.10), channel_id=1, source_target_pairs={{1,0},{0,1},{3,2},{2,3},{5,4},{4,5},{7,6},{6,7},{9,8},{8,9},{11,10... | collective-permute-start | bytes 4208648 | tf_op jit(solution)/shard_map/ppermute | solution.py:295
  68.9 2.6 %copy-start.8 = (bf16[32,1280]{1,0:T(8,128)(2,1)}, bf16[32,1280]{1,0:T(8,128)(2,1)S(1)}, u32[]{:S(2)}) copy-start(bf16[32,1280]{1,0:T(8,128)(2,1)S(1)} %collective-permute-done.11.refs_8_) | copy-start | bytes 245764
  68.9 9.4 %collective-permute-start.15 = (bf16[32,1280]{1,0:T(8,128)(2,1)}, bf16[32,1280]{1,0:T(8,128)(2,1)}, u32[]{:S(2)}, u32[]{:S(2)}) collective-permute-start(bf16[32,1280]{1,0:T(8,128)(2,1)} %get-tuple-element.34), channel_id=1, source_target_pairs={{0,24},{2,26},{4,28},{6,30},{8,16},{10,18},{12,20},{14,22},{16,8},... | collective-permute-start | bytes 245768 | tf_op jit(solution)/shard_map/ppermute | solution.py:234
  72.1 27.2 %collective-permute-start.1 = (bf16[32,3840]{1,0:T(8,128)(2,1)}, bf16[32,3840]{1,0:T(8,128)(2,1)S(1)}, u32[]{:S(2)}, u32[]{:S(2)}) collective-permute-start(bf16[32,3840]{1,0:T(8,128)(2,1)} %get-tuple-element.21), channel_id=1, source_target_pairs={{0,2},{2,0},{4,6},{6,4},{8,10},{10,8},{12,14},{14,12},{16,18},{18,... | collective-permute-start | bytes 737288 | tf_op jit(solution)/shard_map/ppermute | solution.py:234
  73.0 28.4 %collective-permute-start.2 = (bf16[32,3840]{1,0:T(8,128)(2,1)}, bf16[32,3840]{1,0:T(8,128)(2,1)S(1)}, u32[]{:S(2)}, u32[]{:S(2)}) collective-permute-start(bf16[32,3840]{1,0:T(8,128)(2,1)} %get-tuple-element.22), channel_id=1, source_target_pairs={{0,4},{2,6},{4,0},{6,2},{8,12},{10,14},{12,8},{14,10},{16,20},{18,... | collective-permute-start | bytes 737288 | tf_op jit(solution)/shard_map/ppermute | solution.py:234
  75.7 25.7 %collective-permute-start.3 = (bf16[32,3840]{1,0:T(8,128)(2,1)}, bf16[32,3840]{1,0:T(8,128)(2,1)S(1)}, u32[]{:S(2)}, u32[]{:S(2)}) collective-permute-start(bf16[32,3840]{1,0:T(8,128)(2,1)} %get-tuple-element.23), channel_id=1, source_target_pairs={{0,6},{2,4},{4,2},{6,0},{8,14},{10,12},{12,10},{14,8},{16,22},{18,... | collective-permute-start | bytes 737288 | tf_op jit(solution)/shard_map/ppermute | solution.py:234
  78.3 6.7 %collective-permute-start.16 = (bf16[32,1280]{1,0:T(8,128)(2,1)}, bf16[32,1280]{1,0:T(8,128)(2,1)S(1)}, u32[]{:S(2)}, u32[]{:S(2)}) collective-permute-start(bf16[32,1280]{1,0:T(8,128)(2,1)} %get-tuple-element.35), channel_id=1, source_target_pairs={{0,26},{2,24},{4,30},{6,28},{8,18},{10,16},{12,22},{14,20},{16,10}... | collective-permute-start | bytes 245768 | tf_op jit(solution)/shard_map/ppermute | solution.py:234
  85.0 13.8 %copy-start.12 = (bf16[32,1280]{1,0:T(8,128)(2,1)}, bf16[32,1280]{1,0:T(8,128)(2,1)S(1)}, u32[]{:S(2)}) copy-start(bf16[32,1280]{1,0:T(8,128)(2,1)S(1)} %collective-permute-done.16.refs_13_) | copy-start | bytes 245764
  85.0 6.7 %collective-permute-start.17 = (bf16[32,1280]{1,0:T(8,128)(2,1)}, bf16[32,1280]{1,0:T(8,128)(2,1)S(1)}, u32[]{:S(2)}, u32[]{:S(2)}) collective-permute-start(bf16[32,1280]{1,0:T(8,128)(2,1)} %get-tuple-element.36), channel_id=1, source_target_pairs={{0,28},{2,30},{4,24},{6,26},{8,20},{10,22},{12,16},{14,18},{16,12}... | collective-permute-start | bytes 245768 | tf_op jit(solution)/shard_map/ppermute | solution.py:234
  91.6 7.1 %copy-start.13 = (bf16[32,1280]{1,0:T(8,128)(2,1)}, bf16[32,1280]{1,0:T(8,128)(2,1)S(1)}, u32[]{:S(2)}) copy-start(bf16[32,1280]{1,0:T(8,128)(2,1)S(1)} %collective-permute-done.17.refs_14_) | copy-start | bytes 245764
  91.6 7.1 %collective-permute-start.18 = (bf16[32,1280]{1,0:T(8,128)(2,1)}, bf16[32,1280]{1,0:T(8,128)(2,1)S(1)}, u32[]{:S(2)}, u32[]{:S(2)}) collective-permute-start(bf16[32,1280]{1,0:T(8,128)(2,1)} %get-tuple-element.37), channel_id=1, source_target_pairs={{0,30},{2,28},{4,26},{6,24},{8,22},{10,20},{12,18},{14,16},{16,14}... | collective-permute-start | bytes 245768 | tf_op jit(solution)/shard_map/ppermute | solution.py:234
  99.4 7.9 %collective-permute-start.4 = (bf16[32,3840]{1,0:T(8,128)(2,1)}, bf16[32,3840]{1,0:T(8,128)(2,1)S(1)}, u32[]{:S(2)}, u32[]{:S(2)}) collective-permute-start(bf16[32,3840]{1,0:T(8,128)(2,1)} %get-tuple-element.24), channel_id=1, source_target_pairs={{0,8},{2,10},{4,12},{6,14},{8,0},{10,2},{12,4},{14,6},{16,24},{18,... | collective-permute-start | bytes 737288 | tf_op jit(solution)/shard_map/ppermute | solution.py:234
  99.4 7.9 %copy-start.2 = (bf16[32,3840]{1,0:T(8,128)(2,1)}, bf16[32,3840]{1,0:T(8,128)(2,1)S(1)}, u32[]{:S(2)}) copy-start(bf16[32,3840]{1,0:T(8,128)(2,1)S(1)} %collective-permute-done.1.refs_1_) | copy-start | bytes 737284
  99.4 14.1 %collective-permute-start.5 = (bf16[32,3840]{1,0:T(8,128)(2,1)}, bf16[32,3840]{1,0:T(8,128)(2,1)}, u32[]{:S(2)}, u32[]{:S(2)}) collective-permute-start(bf16[32,3840]{1,0:T(8,128)(2,1)} %get-tuple-element.25), channel_id=1, source_target_pairs={{0,10},{2,8},{4,14},{6,12},{8,2},{10,0},{12,6},{14,4},{16,26},{18,... | collective-permute-start | bytes 737288 | tf_op jit(solution)/shard_map/ppermute | solution.py:234
  101.4 5.9 %copy-start.3 = (bf16[32,3840]{1,0:T(8,128)(2,1)}, bf16[32,3840]{1,0:T(8,128)(2,1)S(1)}, u32[]{:S(2)}) copy-start(bf16[32,3840]{1,0:T(8,128)(2,1)S(1)} %collective-permute-done.2.refs_2_) | copy-start | bytes 737284
  101.4 15.9 %collective-permute-start.6 = (bf16[32,3840]{1,0:T(8,128)(2,1)}, bf16[32,3840]{1,0:T(8,128)(2,1)}, u32[]{:S(2)}, u32[]{:S(2)}) collective-permute-start(bf16[32,3840]{1,0:T(8,128)(2,1)} %get-tuple-element.26), channel_id=1, source_target_pairs={{0,12},{2,14},{4,8},{6,10},{8,4},{10,6},{12,0},{14,2},{16,28},{18,... | collective-permute-start | bytes 737288 | tf_op jit(solution)/shard_map/ppermute | solution.py:234
  101.4 5.9 %copy-start.4 = (bf16[32,3840]{1,0:T(8,128)(2,1)}, bf16[32,3840]{1,0:T(8,128)(2,1)S(1)}, u32[]{:S(2)}) copy-start(bf16[32,3840]{1,0:T(8,128)(2,1)S(1)} %collective-permute-done.3.refs_3_) | copy-start | bytes 737284
  101.4 21.7 %collective-permute-start.7 = (bf16[32,3840]{1,0:T(8,128)(2,1)}, bf16[32,3840]{1,0:T(8,128)(2,1)}, u32[]{:S(2)}, u32[]{:S(2)}) collective-permute-start(bf16[32,3840]{1,0:T(8,128)(2,1)} %get-tuple-element.27), channel_id=1, source_target_pairs={{0,14},{2,12},{4,10},{6,8},{8,6},{10,4},{12,2},{14,0},{16,30},{18,... | collective-permute-start | bytes 737288 | tf_op jit(solution)/shard_map/ppermute | solution.py:234
  107.3 15.8 %copy-start.5 = (bf16[32,3840]{1,0:T(8,128)(2,1)}, bf16[32,3840]{1,0:T(8,128)(2,1)S(1)}, u32[]{:S(2)}) copy-start(bf16[32,3840]{1,0:T(8,128)(2,1)S(1)} %collective-permute-done.4.refs_4_) | copy-start | bytes 737284
  (7 other events, 5.6 us)
